TPU v7x, 32 devices: a whole 2x2x4 slice. The times are simulated.
32 devices in a mesh: dom: 8 (over z, y), edge: 4 (over x, core).
Axes of the slice: x: 2, y: 2, z: 4, core: 2. Of those that a mesh axis runs over, the one named last changes fastest.
Arguments:
- embeddings: float32 [4096, 400], P(('dom', 'edge')), may hold values from -1.2 to 1.2
- adagrad_state: float32 [4096], P(('dom', 'edge')), may hold values from 0.01 to 1
- relations: bfloat16 [256, 400], replicated, may hold values from -4 to 4
- endpoints: int32 [2, 2, 8, 2048], P(None, None, 'dom', 'edge'), may hold values from 0 to 511
- relation_ids: int32 [2, 8, 2048], P(None, 'dom', 'edge'), may hold values from 0 to 255
- negatives: int32 [2, 2, 8, 8, 256], P(None, None, 'dom', 'edge'), may hold values from 0 to 511
- edge_counts: int32 [2, 8, 4], P(None, 'dom', 'edge'), may hold values from 1 to 512, as said below
- plan: int32 [2], replicated, may hold values from 1 to 7, as said below
Outputs:
- new_embeddings: float32 [4096, 400], P(('dom', 'edge'))
- new_state: float32 [4096], P(('dom', 'edge'))
Inputs may be any that keep to these rules, and one draw needn't show every extreme that they name: `edge_counts`: in every round some edge group has all 512 slots live; live slots come first. `plan`: consecutive rounds have different patterns; some round has the pattern 8 - 1.
All inputs are finite; a program needn't handle non-finite values.
Results may differ from a plain program's by a relative error of at most 0.01.
Values may be sent and summed in bfloat16 or wider, within the bound.
No kernel may reach another device: no remote copies, remote signals or barrier semaphores. Data moves between devices by JAX's collectives and lax.ppermute only.
A program may use at most 64 MiB of HBM per device.

v0:
```python
import jax
import jax.numpy as jnp
from jax import lax
from jax.sharding import PartitionSpec as P

learning_rate = 0.2


def partner(value, axis, bit):
    mask = 2**bit
    pairs = [(source, source ^ mask) for source in range(lax.axis_size(axis))]
    return lax.ppermute(value, axis, pairs)


def complex_product(left, right):
    half = left.shape[-1] // 2
    left_real, left_imag = (left[..., :half], left[..., half:])
    right_real, right_imag = (right[..., :half], right[..., half:])
    return jnp.concatenate(
        [
            left_real * right_real - left_imag * right_imag,
            left_real * right_imag + left_imag * right_real,
        ],
        axis=-1,
    )


def conjugate(values):
    half = values.shape[-1] // 2
    return jnp.concatenate([values[..., :half], -values[..., half:]], axis=-1)


def bit_isset(mask_value, bit_number):
    return jnp.right_shift(mask_value, bit_number) & 1 == 1


def to_partner(values, mask_value, order):
    for bit_number in order:
        swapped = partner(values, "dom", bit_number)
        values = jnp.where(bit_isset(mask_value, bit_number), swapped, values)
    return values


def from_partner(values, mask_value, order):
    for bit_number in order:
        swapped = partner(values, "dom", bit_number)
        values = jnp.where(bit_isset(mask_value, bit_number), swapped, values)
    return values


def onehot_rows(indices, count):
    return (indices[:, None] == jnp.arange(count, dtype=jnp.int32)[None, :]).astype(jnp.bfloat16)


def transposed_product(onehot, values):
    return lax.dot_general(
        onehot, values, (((0,), (0,)), ((), ())), preferred_element_type=jnp.float32
    )


def bucket_terms(
    full_own, full_partner, relations, lhs_ids, rhs_ids, rel_ids, neg_lhs, neg_rhs, count
):
    part_rows, width = full_own.shape
    edge_slots = lhs_ids.shape[0]
    blocks, negs = neg_lhs.shape
    block_rows = edge_slots // blocks
    onehot_lhs = onehot_rows(lhs_ids, part_rows)
    onehot_rhs = onehot_rows(rhs_ids, part_rows)
    onehot_neg_lhs = onehot_rows(neg_lhs.reshape(-1), part_rows)
    onehot_neg_rhs = onehot_rows(neg_rhs.reshape(-1), part_rows)
    onehot_rel = onehot_rows(rel_ids, relations.shape[0])
    lhs = jnp.dot(onehot_lhs, full_own, preferred_element_type=jnp.float32)
    rhs = jnp.dot(onehot_rhs, full_partner, preferred_element_type=jnp.float32)
    rel = jnp.dot(onehot_rel, relations, preferred_element_type=jnp.float32)
    neg_lhs_rows = (
        jnp.dot(onehot_neg_lhs, full_own, preferred_element_type=jnp.float32)
        .astype(jnp.bfloat16)
        .reshape(blocks, negs, width)
    )
    neg_rhs_rows = (
        jnp.dot(onehot_neg_rhs, full_partner, preferred_element_type=jnp.float32)
        .astype(jnp.bfloat16)
        .reshape(blocks, negs, width)
    )
    queries = complex_product(lhs, rel).astype(jnp.bfloat16)
    backs = complex_product(conjugate(rel), rhs).astype(jnp.bfloat16)
    query_float = queries.astype(jnp.float32)
    positive = jnp.sum(query_float * rhs, axis=-1)
    query_blocks = queries.reshape(blocks, block_rows, width)
    back_blocks = backs.reshape(blocks, block_rows, width)
    scores_rhs = jnp.einsum(
        "cqd,cnd->cqn", query_blocks, neg_rhs_rows, preferred_element_type=jnp.float32
    )
    scores_lhs = jnp.einsum(
        "cqd,cnd->cqn", back_blocks, neg_lhs_rows, preferred_element_type=jnp.float32
    )
    live = (jnp.arange(edge_slots, dtype=jnp.int32) < count).astype(jnp.float32)
    live_blocks = live.reshape(blocks, block_rows, 1)
    weight_pos = -jax.nn.sigmoid(-positive) * live
    weight_rhs = (jax.nn.sigmoid(scores_rhs) * live_blocks * (0.5 / negs)).astype(jnp.bfloat16)
    weight_lhs = (jax.nn.sigmoid(scores_lhs) * live_blocks * (0.5 / negs)).astype(jnp.bfloat16)
    grad_query = weight_pos[:, None] * rhs + jnp.einsum(
        "cqn,cnd->cqd", weight_rhs, neg_rhs_rows, preferred_element_type=jnp.float32
    ).reshape(edge_slots, width)
    grad_back = jnp.einsum(
        "cqn,cnd->cqd", weight_lhs, neg_lhs_rows, preferred_element_type=jnp.float32
    ).reshape(edge_slots, width)
    grad_lhs = complex_product(grad_query, conjugate(rel)).astype(jnp.bfloat16)
    grad_rhs = (weight_pos[:, None] * query_float + complex_product(grad_back, rel)).astype(
        jnp.bfloat16
    )
    grad_neg_rhs = (
        jnp.einsum("cqn,cqd->cnd", weight_rhs, query_blocks, preferred_element_type=jnp.float32)
        .astype(jnp.bfloat16)
        .reshape(-1, width)
    )
    grad_neg_lhs = (
        jnp.einsum("cqn,cqd->cnd", weight_lhs, back_blocks, preferred_element_type=jnp.float32)
        .astype(jnp.bfloat16)
        .reshape(-1, width)
    )
    own_part = transposed_product(onehot_lhs, grad_lhs) + transposed_product(
        onehot_neg_lhs, grad_neg_lhs
    )
    other_part = transposed_product(onehot_rhs, grad_rhs) + transposed_product(
        onehot_neg_rhs, grad_neg_rhs
    )
    return (own_part, other_part)


def on_device(
    embeddings, adagrad_state, relations, endpoints, relation_ids, negatives, edge_counts, plan
):
    bit_count = lax.axis_size("dom").bit_length() - 1
    order = list(range(bit_count))
    table = embeddings
    state = adagrad_state
    for round_index in range(plan.shape[0]):
        mask_value = plan[round_index]
        own_rounded = table.astype(jnp.bfloat16)
        partner_rounded = to_partner(own_rounded, mask_value, order)
        full_own, full_partner = (
            lax.all_gather(own_rounded, "edge", axis=0, tiled=True),
            lax.all_gather(partner_rounded, "edge", axis=0, tiled=True),
        )
        own_part, other_part = bucket_terms(
            full_own,
            full_partner,
            relations,
            endpoints[round_index, 0, 0],
            endpoints[round_index, 1, 0],
            relation_ids[round_index, 0],
            negatives[round_index, 0, 0],
            negatives[round_index, 1, 0],
            edge_counts[round_index, 0, 0],
        )
        own_share, other_share = (
            lax.psum_scatter(
                own_part.astype(jnp.bfloat16), "edge", scatter_dimension=0, tiled=True
            ).astype(jnp.float32),
            lax.psum_scatter(
                other_part.astype(jnp.bfloat16), "edge", scatter_dimension=0, tiled=True
            ).astype(jnp.float32),
        )
        returned = from_partner(other_share.astype(jnp.bfloat16), mask_value, order).astype(
            jnp.float32
        )
        total = own_share + returned
        state = state + jnp.mean(total * total, axis=1)
        table = table - learning_rate * total / jnp.sqrt(state)[:, None]
    return (table, state)


def solution(mesh):
    in_specs = (
        P(("dom", "edge"), None),
        P(("dom", "edge")),
        P(),
        P(None, None, "dom", "edge"),
        P(None, "dom", "edge"),
        P(None, None, "dom", "edge", None),
        P(None, "dom", "edge"),
        P(),
    )
    out_specs = (P(("dom", "edge"), None), P(("dom", "edge")))
    return jax.shard_map(
        on_device, mesh=mesh, in_specs=in_specs, out_specs=out_specs, check_vma=False
    )
```

profile of v0, /device:TPU:0, one launch (start us, length us, event | category | flops | bytes accessed | tf_op | source)
XLA Modules:
  0.0 185.6 jit_solution(14794494941252523609)
XLA Ops:
  7.2 1.0 convert_element_type.116
  8.2 3.1 %collective-permute-start = (bf16[128,400]{0,1:T(8,128)(2,1)S(1)}, bf16[128,400]{0,1:T(8,128)(2,1)S(1)}, u32[]{:S(2)}, u32[]{:S(2)}) collective-permute-start(bf16[128,400]{0,1:T(8,128)(2,1)S(1)} %convert_element_type.116), channel_id=1, source_target_pairs={{0,4},{4,0},{8,12},{12,8},{16,20},{20,16},{24,28},{28,24},{1,5},{5... | collective-permute-start | bytes 307208 | tf_op jit(solution)/shard_map/ppermute | solution.py:12
  11.3 6.6 %all_gather.12 = bf16[512,400]{0,1:T(8,128)(2,1)S(1)} all-gather(bf16[128,400]{0,1:T(8,128)(2,1)S(1)} %convert_element_type.116), channel_id=1, replica_groups=mesh['dom'=8,'edge'=4] {'edge'}, dimensions={0}, use_global_device_ids=true | all-gather | bytes 512000 | tf_op jit(solution)/shard_map/all_gather | solution.py:144
  17.9 0.7 copy-done.4
  18.6 0.7 copy-done.3
  19.8 0.5 convolution_convert_fusion.6
  21.0 0.6 fusion.104
  23.6 1.6 collective-permute-start.1
  25.3 0.6 fusion.103
  25.9 3.0 %collective-permute-done.1 = bf16[128,400]{0,1:T(8,128)(2,1)S(1)} collective-permute-done((bf16[128,400]{0,1:T(8,128)(2,1)S(1)}, bf16[128,400]{0,1:T(8,128)(2,1)S(1)}, u32[]{:S(2)}, u32[]{:S(2)}) %collective-permute-start.1) | collective-permute-done | bytes 102432 | tf_op jit(solution)/shard_map/ppermute | solution.py:12
  28.8 2.7 %collective-permute-start.2 = (bf16[128,400]{0,1:T(8,128)(2,1)S(1)}, bf16[128,400]{0,1:T(8,128)(2,1)S(1)}, u32[]{:S(2)}, u32[]{:S(2)}) collective-permute-start(bf16[128,400]{0,1:T(8,128)(2,1)S(1)} %broadcast_select_fusion.9), channel_id=1, source_target_pairs={{0,16},{4,20},{8,24},{12,28},{16,0},{20,4},{24,8},{28,12},{1,17},{... | collective-permute-start | bytes 307208 | tf_op jit(solution)/shard_map/ppermute | solution.py:12
  31.5 0.6 compare_convert_fusion.1
  32.1 4.2 %collective-permute-done.2 = bf16[128,400]{0,1:T(8,128)(2,1)S(1)} collective-permute-done((bf16[128,400]{0,1:T(8,128)(2,1)S(1)}, bf16[128,400]{0,1:T(8,128)(2,1)S(1)}, u32[]{:S(2)}, u32[]{:S(2)}) %collective-permute-start.2) | collective-permute-done | bytes 102432 | tf_op jit(solution)/shard_map/ppermute | solution.py:12
  36.3 6.2 %all_gather.13 = bf16[512,400]{0,1:T(8,128)(2,1)S(1)} all-gather(bf16[128,400]{0,1:T(8,128)(2,1)S(1)} %broadcast_select_fusion.11), channel_id=1, replica_groups=mesh['dom'=8,'edge'=4] {'edge'}, dimensions={0}, use_global_device_ids=true | all-gather | bytes 512000 | tf_op jit(solution)/shard_map/all_gather | solution.py:145
  45.3 0.6 negate_select_fusion.1
  48.3 1.0 copy.80
  50.2 20.8 %reduce-scatter.15.cloned.1.call-done = bf16[128,400]{1,0:T(8,128)(2,1)} async-done(((bf16[512,400]{1,0:T(8,128)(2,1)}), bf16[128,400]{1,0:T(8,128)(2,1)}) %reduce-scatter.15.cloned.1.call-update) | async-done | bytes 102416
  70.9 1.0 copy.81
  72.0 1.5 collective-permute-start.3
  74.0 1.0 copy.78
  75.1 1.6 collective-permute-done.3
  76.7 1.6 collective-permute-start.4
  80.6 0.8 collective-permute-done.4
  81.5 2.5 %collective-permute-start.5 = (bf16[128,400]{0,1:T(8,128)(2,1)S(1)}, bf16[128,400]{0,1:T(8,128)(2,1)S(1)}, u32[]{:S(2)}, u32[]{:S(2)}) collective-permute-start(bf16[128,400]{0,1:T(8,128)(2,1)S(1)} %broadcast_select_fusion.8), channel_id=1, source_target_pairs={{0,16},{4,20},{8,24},{12,28},{16,0},{20,4},{24,8},{28,12},{1,17},{... | collective-permute-start | bytes 307208 | tf_op jit(solution)/shard_map/ppermute | solution.py:12
  83.9 0.7 compare_convert_fusion
  84.6 11.4 %reduce-scatter.13.cloned.1.call-done = bf16[128,400]{1,0:T(8,128)(2,1)} async-done(((bf16[512,400]{1,0:T(8,128)(2,1)}), bf16[128,400]{1,0:T(8,128)(2,1)}) %reduce-scatter.13.cloned.1.call-update) | async-done | bytes 102416
  96.0 1.0 copy.79
  97.1 0.6 copy-done.7
  97.7 1.5 collective-permute-start.6
  99.3 6.2 %all_gather.14 = bf16[512,400]{0,1:T(8,128)(2,1)S(1)} all-gather(bf16[128,400]{0,1:T(8,128)(2,1)S(1)} %fusion.99), channel_id=1, replica_groups=mesh['dom'=8,'edge'=4] {'edge'}, dimensions={0}, use_global_device_ids=true | all-gather | bytes 512000 | tf_op jit(solution)/shard_map/all_gather | solution.py:144
  105.5 1.6 collective-permute-start.7
  107.6 3.1 %collective-permute-done.7 = bf16[128,400]{0,1:T(8,128)(2,1)S(1)} collective-permute-done((bf16[128,400]{0,1:T(8,128)(2,1)S(1)}, bf16[128,400]{0,1:T(8,128)(2,1)S(1)}, u32[]{:S(2)}, u32[]{:S(2)}) %collective-permute-start.7) | collective-permute-done | bytes 102432 | tf_op jit(solution)/shard_map/ppermute | solution.py:12
  110.7 2.5 %collective-permute-start.8 = (bf16[128,400]{0,1:T(8,128)(2,1)S(1)}, bf16[128,400]{0,1:T(8,128)(2,1)S(1)}, u32[]{:S(2)}, u32[]{:S(2)}) collective-permute-start(bf16[128,400]{0,1:T(8,128)(2,1)S(1)} %broadcast_select_fusion.3), channel_id=1, source_target_pairs={{0,16},{4,20},{8,24},{12,28},{16,0},{20,4},{24,8},{28,12},{1,17},{... | collective-permute-start | bytes 307208 | tf_op jit(solution)/shard_map/ppermute | solution.py:12
  113.7 4.4 %collective-permute-done.8 = bf16[128,400]{0,1:T(8,128)(2,1)S(1)} collective-permute-done((bf16[128,400]{0,1:T(8,128)(2,1)S(1)}, bf16[128,400]{0,1:T(8,128)(2,1)S(1)}, u32[]{:S(2)}, u32[]{:S(2)}) %collective-permute-start.8) | collective-permute-done | bytes 102432 | tf_op jit(solution)/shard_map/ppermute | solution.py:12
  118.1 6.4 %all_gather.15 = bf16[512,400]{0,1:T(8,128)(2,1)S(1)} all-gather(bf16[128,400]{0,1:T(8,128)(2,1)S(1)} %broadcast_select_fusion.5), channel_id=1, replica_groups=mesh['dom'=8,'edge'=4] {'edge'}, dimensions={0}, use_global_device_ids=true | all-gather | bytes 512000 | tf_op jit(solution)/shard_map/all_gather | solution.py:145
  127.2 0.7 negate_select_fusion
  130.4 1.0 copy.84
  132.8 1.0 copy.82
  133.9 18.8 %reduce-scatter.19.cloned.1.call-done = bf16[128,400]{1,0:T(8,128)(2,1)} async-done(((bf16[512,400]{1,0:T(8,128)(2,1)}), bf16[128,400]{1,0:T(8,128)(2,1)}) %reduce-scatter.19.cloned.1.call-update) | async-done | bytes 102416
  152.7 1.0 copy.85
  153.7 1.5 collective-permute-start.9
  155.2 3.2 %collective-permute-done.9 = bf16[128,400]{0,1:T(8,128)(2,1)S(1)} collective-permute-done((bf16[128,400]{0,1:T(8,128)(2,1)S(1)}, bf16[128,400]{0,1:T(8,128)(2,1)S(1)}, u32[]{:S(2)}, u32[]{:S(2)}) %collective-permute-start.9) | collective-permute-done | bytes 102432 | tf_op jit(solution)/shard_map/ppermute | solution.py:12
  158.4 1.5 collective-permute-start.10
  160.0 3.2 %collective-permute-done.10 = bf16[128,400]{0,1:T(8,128)(2,1)S(1)} collective-permute-done((bf16[128,400]{0,1:T(8,128)(2,1)S(1)}, bf16[128,400]{0,1:T(8,128)(2,1)S(1)}, u32[]{:S(2)}, u32[]{:S(2)}) %collective-permute-start.10) | collective-permute-done | bytes 102432 | tf_op jit(solution)/shard_map/ppermute | solution.py:12
  163.2 2.5 %collective-permute-start.11 = (bf16[128,400]{0,1:T(8,128)(2,1)S(1)}, bf16[128,400]{0,1:T(8,128)(2,1)S(1)}, u32[]{:S(2)}, u32[]{:S(2)}) collective-permute-start(bf16[128,400]{0,1:T(8,128)(2,1)S(1)} %broadcast_select_fusion.2), channel_id=1, source_target_pairs={{0,16},{4,20},{8,24},{12,28},{16,0},{20,4},{24,8},{28,12},{1,17},{... | collective-permute-start | bytes 307208 | tf_op jit(solution)/shard_map/ppermute | solution.py:12
  165.6 11.0 %reduce-scatter.17.cloned.1.call-done = bf16[128,400]{1,0:T(8,128)(2,1)} async-done(((bf16[512,400]{1,0:T(8,128)(2,1)}), bf16[128,400]{1,0:T(8,128)(2,1)}) %reduce-scatter.17.cloned.1.call-update) | async-done | bytes 102416
  176.7 1.0 copy.83
  178.3 0.8 divide_subtract_fusion
  (100 shorter events, 16.5 us)
Async XLA Ops:
  7.2 13.2 %copy-start = (bf16[256,400]{0,1:T(8,128)(2,1)S(1)}, bf16[256,400]{0,1:T(8,128)(2,1)}, u32[]{:S(2)}) copy-start(bf16[256,400]{0,1:T(8,128)(2,1)} %param.10) | copy-start | bytes 614404
  7.2 63.8 %reduce-scatter.15.cloned.1.call-start = ((), (), s32[]{:S(2)}) async-start(), calls=%async_computation.5 | async-start | bytes 655360
  8.2 9.6 %copy-start.2 = (s32[2,2,1,512]{3,2,1,0:T(1,128)S(1)}, s32[2,2,1,512]{3,2,1,0:T(1,128)}, u32[]{:S(2)}) copy-start(s32[2,2,1,512]{3,2,1,0:T(1,128)} %param.11) | copy-start | bytes 24580
  8.2 15.3 %collective-permute-start = (bf16[128,400]{0,1:T(8,128)(2,1)S(1)}, bf16[128,400]{0,1:T(8,128)(2,1)S(1)}, u32[]{:S(2)}, u32[]{:S(2)}) collective-permute-start(bf16[128,400]{0,1:T(8,128)(2,1)S(1)} %convert_element_type.116), channel_id=1, source_target_pairs={{0,4},{4,0},{8,12},{12,8},{16,20},{20,16},{24,28},{28,24},{1,5},{5... | collective-permute-start | bytes 307208 | tf_op jit(solution)/shard_map/ppermute | solution.py:12
  17.9 0.7 copy-start.4
  18.5 0.7 copy-start.3
  20.4 0.7 copy-start.5
  20.4 3.2 %copy-start.1 = (f32[128,400]{0,1:T(8,128)S(1)}, f32[128,400]{0,1:T(8,128)}, u32[]{:S(2)}) copy-start(f32[128,400]{0,1:T(8,128)} %param.8) | copy-start | bytes 614404
  23.6 1.7 copy-start.6
  23.6 5.2 %collective-permute-start.1 = (bf16[128,400]{0,1:T(8,128)(2,1)S(1)}, bf16[128,400]{0,1:T(8,128)(2,1)S(1)}, u32[]{:S(2)}, u32[]{:S(2)}) collective-permute-start(bf16[128,400]{0,1:T(8,128)(2,1)S(1)} %broadcast_select_fusion.7), channel_id=1, source_target_pairs={{0,8},{4,12},{8,0},{12,4},{16,24},{20,28},{24,16},{28,20},{1,9},{5... | collective-permute-start | bytes 307208 | tf_op jit(solution)/shard_map/ppermute | solution.py:12
  28.8 7.4 %collective-permute-start.2 = (bf16[128,400]{0,1:T(8,128)(2,1)S(1)}, bf16[128,400]{0,1:T(8,128)(2,1)S(1)}, u32[]{:S(2)}, u32[]{:S(2)}) collective-permute-start(bf16[128,400]{0,1:T(8,128)(2,1)S(1)} %broadcast_select_fusion.9), channel_id=1, source_target_pairs={{0,16},{4,20},{8,24},{12,28},{16,0},{20,4},{24,8},{28,12},{1,17},{... | collective-permute-start | bytes 307208 | tf_op jit(solution)/shard_map/ppermute | solution.py:12
  49.3 46.6 %reduce-scatter.13.cloned.1.call-start = ((), (), s32[]{:S(2)}) async-start(), calls=%async_computation.4 | async-start | bytes 655360
  72.0 4.7 %collective-permute-start.3 = (bf16[128,400]{0,1:T(8,128)(2,1)S(1)}, bf16[128,400]{0,1:T(8,128)(2,1)S(1)}, u32[]{:S(2)}, u32[]{:S(2)}) collective-permute-start(bf16[128,400]{0,1:T(8,128)(2,1)S(1)} %copy.81), channel_id=1, source_target_pairs={{0,4},{4,0},{8,12},{12,8},{16,20},{20,16},{24,28},{28,24},{1,5},{5... | collective-permute-start | bytes 307208 | tf_op jit(solution)/shard_map/ppermute | solution.py:12
  75.1 77.6 %reduce-scatter.19.cloned.1.call-start = ((), (), s32[]{:S(2)}) async-start(), calls=%async_computation.7 | async-start | bytes 655360
  76.7 4.7 %collective-permute-start.4 = (bf16[128,400]{0,1:T(8,128)(2,1)S(1)}, bf16[128,400]{0,1:T(8,128)(2,1)S(1)}, u32[]{:S(2)}, u32[]{:S(2)}) collective-permute-start(bf16[128,400]{0,1:T(8,128)(2,1)S(1)} %broadcast_select_fusion.6), channel_id=1, source_target_pairs={{0,8},{4,12},{8,0},{12,4},{16,24},{20,28},{24,16},{28,20},{1,9},{5... | collective-permute-start | bytes 307208 | tf_op jit(solution)/shard_map/ppermute | solution.py:12
  81.5 15.5 %collective-permute-start.5 = (bf16[128,400]{0,1:T(8,128)(2,1)S(1)}, bf16[128,400]{0,1:T(8,128)(2,1)S(1)}, u32[]{:S(2)}, u32[]{:S(2)}) collective-permute-start(bf16[128,400]{0,1:T(8,128)(2,1)S(1)} %broadcast_select_fusion.8), channel_id=1, source_target_pairs={{0,16},{4,20},{8,24},{12,28},{16,0},{20,4},{24,8},{28,12},{1,17},{... | collective-permute-start | bytes 307208 | tf_op jit(solution)/shard_map/ppermute | solution.py:12
  97.0 0.7 copy-start.7
  97.7 7.7 %collective-permute-start.6 = (bf16[128,400]{0,1:T(8,128)(2,1)S(1)}, bf16[128,400]{0,1:T(8,128)(2,1)S(1)}, u32[]{:S(2)}, u32[]{:S(2)}) collective-permute-start(bf16[128,400]{0,1:T(8,128)(2,1)S(1)} %fusion.99), channel_id=1, source_target_pairs={{0,4},{4,0},{8,12},{12,8},{16,20},{20,16},{24,28},{28,24},{1,5},{5... | collective-permute-start | bytes 307208 | tf_op jit(solution)/shard_map/ppermute | solution.py:12
  105.5 5.2 %collective-permute-start.7 = (bf16[128,400]{0,1:T(8,128)(2,1)S(1)}, bf16[128,400]{0,1:T(8,128)(2,1)S(1)}, u32[]{:S(2)}, u32[]{:S(2)}) collective-permute-start(bf16[128,400]{0,1:T(8,128)(2,1)S(1)} %broadcast_select_fusion.1), channel_id=1, source_target_pairs={{0,8},{4,12},{8,0},{12,4},{16,24},{20,28},{24,16},{28,20},{1,9},{5... | collective-permute-start | bytes 307208 | tf_op jit(solution)/shard_map/ppermute | solution.py:12
  110.7 7.4 %collective-permute-start.8 = (bf16[128,400]{0,1:T(8,128)(2,1)S(1)}, bf16[128,400]{0,1:T(8,128)(2,1)S(1)}, u32[]{:S(2)}, u32[]{:S(2)}) collective-permute-start(bf16[128,400]{0,1:T(8,128)(2,1)S(1)} %broadcast_select_fusion.3), channel_id=1, source_target_pairs={{0,16},{4,20},{8,24},{12,28},{16,0},{20,4},{24,8},{28,12},{1,17},{... | collective-permute-start | bytes 307208 | tf_op jit(solution)/shard_map/ppermute | solution.py:12
  131.4 45.2 %reduce-scatter.17.cloned.1.call-start = ((), (), s32[]{:S(2)}) async-start(), calls=%async_computation.6 | async-start | bytes 655360
  153.7 4.7 %collective-permute-start.9 = (bf16[128,400]{0,1:T(8,128)(2,1)S(1)}, bf16[128,400]{0,1:T(8,128)(2,1)S(1)}, u32[]{:S(2)}, u32[]{:S(2)}) collective-permute-start(bf16[128,400]{0,1:T(8,128)(2,1)S(1)} %copy.85), channel_id=1, source_target_pairs={{0,4},{4,0},{8,12},{12,8},{16,20},{20,16},{24,28},{28,24},{1,5},{5... | collective-permute-start | bytes 307208 | tf_op jit(solution)/shard_map/ppermute | solution.py:12
  158.4 4.7 %collective-permute-start.10 = (bf16[128,400]{0,1:T(8,128)(2,1)S(1)}, bf16[128,400]{0,1:T(8,128)(2,1)S(1)}, u32[]{:S(2)}, u32[]{:S(2)}) collective-permute-start(bf16[128,400]{0,1:T(8,128)(2,1)S(1)} %broadcast_select_fusion), channel_id=1, source_target_pairs={{0,8},{4,12},{8,0},{12,4},{16,24},{20,28},{24,16},{28,20},{1,9},{5... | collective-permute-start | bytes 307208 | tf_op jit(solution)/shard_map/ppermute | solution.py:12
  163.2 14.5 %collective-permute-start.11 = (bf16[128,400]{0,1:T(8,128)(2,1)S(1)}, bf16[128,400]{0,1:T(8,128)(2,1)S(1)}, u32[]{:S(2)}, u32[]{:S(2)}) collective-permute-start(bf16[128,400]{0,1:T(8,128)(2,1)S(1)} %broadcast_select_fusion.2), channel_id=1, source_target_pairs={{0,16},{4,20},{8,24},{12,28},{16,0},{20,4},{24,8},{28,12},{1,17},{... | collective-permute-start | bytes 307208 | tf_op jit(solution)/shard_map/ppermute | solution.py:12
Sparse Core Ops, SparseCore 0:
  49.4 21.4 reduce-scatter.14
  75.2 20.7 reduce-scatter.12
  131.6 21.0 reduce-scatter.18
  155.0 21.6 reduce-scatter.16
where the time goes:
time: 186 us
  waiting for transfers between devices  85.5 us (46%)
  blocking collectives  25.4 us (14%)
  starting transfers between devices  24.2 us (13%)
  between operations  18.3 us (10%)
  matrix products  13 us (7%)
  local copies, waits for them, and re-layouts  12.2 us (7%)
  other arithmetic  7.13 us (4%)
    unnamed x8, waiting for transfers between devices  62 us
    ppermute x12, starting transfers between devices, partner(): return lax.ppermute(value, axis, pairs)  24 us
    ppermute x12, waiting for transfers between devices, partner(): return lax.ppermute(value, axis, pairs)  23.5 us
    all_gather x2, blocking collectives, on_device(): lax.all_gather(own_rounded, 'edge', axis=0, tiled=True)  12.8 us
    all_gather x2, blocking collectives, on_device(): lax.all_gather(partner_rounded, 'edge', axis=0, tiled=True)  12.6 us
    unnamed x33, local copies, waits for them, and re-layouts  10.5 us
    dot_general x8, matrix products, transposed_product(): lax.dot_general(onehot, values, (((0,), (0,)), ((), ())), preferred_eleme...  4.01 us
  transfers between devices with their start and end apart: 16, of which 12 were waited for; matrix products, arithmetic and copies ran while one was open for 7% of the time, Pallas kernels for 0%

commit v1 on v0

v1 whole, which is shorter than its diff:
```python
import jax
import jax.numpy as jnp
from jax import lax
from jax.sharding import PartitionSpec as P

learning_rate = 0.2
AXES = ("dom", "edge")
CHUNK_BITS = 3


def exchange(value, dom_mask, edge_mask):
    doms, edges = lax.axis_size("dom"), lax.axis_size("edge")
    pairs = [
        (d * edges + e, (d ^ dom_mask) * edges + (e ^ edge_mask))
        for d in range(doms)
        for e in range(edges)
    ]
    return lax.ppermute(value, AXES, pairs)


def complex_product(left, right):
    half = left.shape[0] // 2
    left_real, left_imag = (left[:half], left[half:])
    right_real, right_imag = (right[:half], right[half:])
    return jnp.concatenate(
        [
            left_real * right_real - left_imag * right_imag,
            left_real * right_imag + left_imag * right_real,
        ],
        axis=0,
    )


def conjugate(values):
    half = values.shape[0] // 2
    return jnp.concatenate([values[:half], -values[half:]], axis=0)


def chunks():
    bits = lax.axis_size("dom").bit_length() - 1
    return [(low, min(CHUNK_BITS, bits - low)) for low in range(0, bits, CHUNK_BITS)]


def gathered(block, mask):
    runs = chunks()
    moved = block
    for low, bits in runs[:-1]:
        field = jnp.right_shift(mask, low) & (2**bits - 1)
        moved = lax.switch(
            field,
            [(lambda v, m=m: exchange(v, m << low, 0) if m else v) for m in range(2**bits)],
            moved,
        )
    low, bits = runs[-1]
    first = 1 if len(runs) == 1 else 0
    field = (jnp.right_shift(mask, low) & (2**bits - 1)) - first
    near, far, cross = lax.switch(
        field,
        [
            (
                lambda v, o, m=m: (
                    exchange(v, m << low, 0) if m else v,
                    exchange(v, m << low, 2),
                    exchange(o, 0, 2),
                )
            )
            for m in range(first, 2**bits)
        ],
        moved,
        block,
    )
    held = jnp.concatenate([block, cross, near, far], axis=1)
    other = exchange(held, 0, 1)
    rows = block.shape[1]
    part = lambda a, i: a[:, i * rows : (i + 1) * rows]
    own = jnp.concatenate([part(held, 0), part(other, 0), part(held, 1), part(other, 1)], axis=1)
    partner = jnp.concatenate(
        [part(held, 2), part(other, 2), part(held, 3), part(other, 3)], axis=1
    )
    return own, partner


def reduced(own_part, other_part, mask):
    rows = own_part.shape[1] // 4
    part = lambda a, i: a[:, i * rows : (i + 1) * rows]
    sent = jnp.concatenate(
        [part(other_part, 1), part(other_part, 3), part(own_part, 1), part(own_part, 3)], axis=1
    ).astype(jnp.bfloat16)
    came = exchange(sent, 0, 1).astype(jnp.float32)
    other_near = (part(other_part, 0) + part(came, 0)).astype(jnp.bfloat16)
    other_far = (part(other_part, 2) + part(came, 1)).astype(jnp.bfloat16)
    own_near = part(own_part, 0) + part(came, 2)
    own_far = (part(own_part, 2) + part(came, 3)).astype(jnp.bfloat16)
    runs = chunks()
    for low, bits in runs[:-1]:
        field = jnp.right_shift(mask, low) & (2**bits - 1)
        other_near, other_far = lax.switch(
            field,
            [
                (lambda a, b, m=m: (exchange(a, m << low, 0), exchange(b, m << low, 0)) if m else (a, b))
                for m in range(2**bits)
            ],
            other_near,
            other_far,
        )
    low, bits = runs[-1]
    first = 1 if len(runs) == 1 else 0
    field = (jnp.right_shift(mask, low) & (2**bits - 1)) - first
    near, far, cross = lax.switch(
        field,
        [
            (
                lambda a, b, c, m=m: (
                    exchange(a, m << low, 0) if m else a,
                    exchange(b, m << low, 2),
                    exchange(c, 0, 2),
                )
            )
            for m in range(first, 2**bits)
        ],
        other_near,
        other_far,
        own_far,
    )
    f32 = jnp.float32
    return own_near + cross.astype(f32) + (near.astype(f32) + far.astype(f32))


def onehot(ids, count):
    return (jnp.arange(count, dtype=jnp.int32)[:, None] == ids[None, :]).astype(jnp.bfloat16)


def dot(a, b):
    return jnp.dot(a, b, preferred_element_type=jnp.float32)


def dot_nt(a, b):
    return lax.dot_general(a, b, (((1,), (1,)), ((), ())), preferred_element_type=jnp.float32)


def dot_tn(a, b):
    return lax.dot_general(a, b, (((0,), (0,)), ((), ())), preferred_element_type=jnp.float32)


def bucket_terms(own, partner, relations, lhs_ids, rhs_ids, rel_ids, neg_lhs, neg_rhs, count):
    bf16 = jnp.bfloat16
    width, part_rows = own.shape
    edge_slots = lhs_ids.shape[0]
    blocks, negs = neg_lhs.shape
    block_rows = edge_slots // blocks
    hot_lhs = onehot(jnp.concatenate([lhs_ids, neg_lhs.reshape(-1)]), part_rows)
    hot_rhs = onehot(jnp.concatenate([rhs_ids, neg_rhs.reshape(-1)]), part_rows)
    hot_rel = onehot(rel_ids, relations.shape[1])
    rows_lhs = dot(own, hot_lhs)
    rows_rhs = dot(partner, hot_rhs)
    rel = dot(relations, hot_rel)
    lhs, neg_lhs_rows = rows_lhs[:, :edge_slots], rows_lhs[:, edge_slots:].astype(bf16)
    rhs, neg_rhs_rows = rows_rhs[:, :edge_slots], rows_rhs[:, edge_slots:].astype(bf16)
    queries = complex_product(lhs, rel).astype(bf16)
    backs = complex_product(conjugate(rel), rhs).astype(bf16)
    query_float = queries.astype(jnp.float32)
    positive = jnp.sum(query_float * rhs, axis=0)
    live = (jnp.arange(edge_slots, dtype=jnp.int32) < count).astype(jnp.float32)
    weight_pos = -jax.nn.sigmoid(-positive) * live
    query_terms, back_terms, grad_neg_rhs, grad_neg_lhs = [], [], [], []
    for c in range(blocks):
        edges = slice(c * block_rows, (c + 1) * block_rows)
        drawn = slice(c * negs, (c + 1) * negs)
        q, b, nr, nl = (queries[:, edges], backs[:, edges], neg_rhs_rows[:, drawn], neg_lhs_rows[:, drawn])
        scale = live[edges][:, None] * (0.5 / negs)
        weight_rhs = (jax.nn.sigmoid(dot_tn(q, nr)) * scale).astype(bf16)
        weight_lhs = (jax.nn.sigmoid(dot_tn(b, nl)) * scale).astype(bf16)
        query_terms.append(dot_nt(nr, weight_rhs))
        back_terms.append(dot_nt(nl, weight_lhs))
        grad_neg_rhs.append(dot(q, weight_rhs).astype(bf16))
        grad_neg_lhs.append(dot(b, weight_lhs).astype(bf16))
    grad_query = weight_pos[None, :] * rhs + jnp.concatenate(query_terms, axis=1)
    grad_back = jnp.concatenate(back_terms, axis=1)
    grad_lhs = complex_product(grad_query, conjugate(rel)).astype(bf16)
    grad_rhs = (weight_pos[None, :] * query_float + complex_product(grad_back, rel)).astype(bf16)
    other_part = dot_nt(jnp.concatenate([grad_rhs] + grad_neg_rhs, axis=1), hot_rhs)
    own_part = dot_nt(jnp.concatenate([grad_lhs] + grad_neg_lhs, axis=1), hot_lhs)
    return own_part, other_part


def on_device(
    embeddings, adagrad_state, relations, endpoints, relation_ids, negatives, edge_counts, plan
):
    rows = embeddings.shape[0]
    slot = lax.axis_index("edge") * rows
    endpoints, negatives = endpoints ^ slot, negatives ^ slot
    table = embeddings.T
    state = adagrad_state
    relations = relations.T
    for round_index in range(plan.shape[0]):
        mask = plan[round_index]
        own, partner = gathered(table.astype(jnp.bfloat16), mask)
        own_part, other_part = bucket_terms(
            own,
            partner,
            relations,
            endpoints[round_index, 0, 0],
            endpoints[round_index, 1, 0],
            relation_ids[round_index, 0],
            negatives[round_index, 0, 0],
            negatives[round_index, 1, 0],
            edge_counts[round_index, 0, 0],
        )
        total = reduced(own_part, other_part, mask)
        state = state + jnp.mean(total * total, axis=0)
        table = table - learning_rate * total / jnp.sqrt(state)[None, :]
    return (table.T, state)


def solution(mesh):
    in_specs = (
        P(("dom", "edge"), None),
        P(("dom", "edge")),
        P(),
        P(None, None, "dom", "edge"),
        P(None, "dom", "edge"),
        P(None, None, "dom", "edge", None),
        P(None, "dom", "edge"),
        P(),
    )
    out_specs = (P(("dom", "edge"), None), P(("dom", "edge")))
    return jax.shard_map(
        on_device, mesh=mesh, in_specs=in_specs, out_specs=out_specs, check_vma=False
    )
```

time: 186 us -> 94.2 us (0.51)
  waiting for transfers between devices: 85.5 us -> 30.7 us
  blocking collectives: 25.4 us -> 0 us
  between operations: 18.3 us -> 2.5 us
  local copies, waits for them, and re-layouts: 12.2 us -> 3.68 us
  other arithmetic: 7.13 us -> 15 us
  matrix products: 13 us -> 15.5 us
  starting transfers between devices: 24.2 us -> 26.5 us
    unnamed x8 -> x0, waiting for transfers between devices: 62 us -> none
    all_gather x4 -> x0, blocking collectives: 25.4 us -> none  [the longest x2 12.8 us: on_device(): lax.all_gather(own_rounded, 'edge', axis=0, tiled=True)]
    unnamed x33 -> x11, local copies, waits for them, and re-layouts: 10.5 us -> 0.04 us
    ppermute x12 -> x16, waiting for transfers between devices: 23.5 us -> 30.7 us  [exchange(): return lax.ppermute(value, AXES, pairs)]
    dot_general x30 -> x34, matrix products: 13 us -> 15.5 us  [the longest x14 8.65 us: dot(): return jnp.dot(a, b, preferred_element_type=jnp.float32)]
    ppermute x12 -> x16, starting transfers between devices: 24 us -> 26.5 us  [exchange(): return lax.ppermute(value, AXES, pairs)]
    concatenate x0 -> x8, other arithmetic: none -> 2.25 us  [the longest x2 2.11 us: gathered(): held = jnp.concatenate([block, cross, near, far], axis=1)]
    reduce_sum x4, other arithmetic: 0.48 us -> 2.34 us  [the longest x2 1.99 us: on_device(): state = state + jnp.mean(total * total, axis=0)]
  transfers between devices with their start and end apart: 16 -> 16, of which waited for: 12 -> 11; matrix products, arithmetic and copies ran while one was open for 7% -> 8% of each run, Pallas kernels for 0% -> 0%
where the time goes in v1:
time: 94.2 us; the launch traced here: 94.1 us
  waiting for transfers between devices  30.7 us (33%)
  starting transfers between devices  26.5 us (28%)
  matrix products  15.5 us (16%)
  other arithmetic  15 us (16%)
  local copies, waits for them, and re-layouts  3.68 us (4%)
  between operations  2.5 us (3%)
    ppermute x16, waiting for transfers between devices, exchange(): return lax.ppermute(value, AXES, pairs)  30.7 us
    ppermute x16, starting transfers between devices, exchange(): return lax.ppermute(value, AXES, pairs)  26.5 us
    dot_general x14, matrix products, dot(): return jnp.dot(a, b, preferred_element_type=jnp.float32)  8.65 us
    dot_general x12, matrix products, dot_nt(): lax.dot_general(a, b, (((1,), (1,)), ((), ())), preferred_element_type=jn...  4.53 us
    dot_general x8, matrix products, dot_tn(): lax.dot_general(a, b, (((0,), (0,)), ((), ())), preferred_element_type=jn...  2.37 us
    concatenate x2, other arithmetic, gathered(): held = jnp.concatenate([block, cross, near, far], axis=1)  2.11 us
    reduce_sum x2, other arithmetic, on_device(): state = state + jnp.mean(total * total, axis=0)  1.99 us
  transfers between devices with their start and end apart: 16, of which 11 were waited for; matrix products, arithmetic and copies ran while one was open for 8% of the time, Pallas kernels for 0%

profile of v1, /device:TPU:0, one launch (start us, length us, event | category | flops | bytes accessed | tf_op | source)
XLA Modules:
  0.0 94.1 jit_solution(14915250485739271289)
XLA Ops:
  0.6 1.0 %bitcast_convert_fusion = bf16[400,128]{1,0:T(8,128)(2,1)S(1)} fusion(f32[128,400]{0,1:T(8,128)} %param.36), kind=kLoop, calls=%fused_computation.231 | loop fusion | flops 51200 | bytes 307200 | tf_op jit(solution)/shard_map/convert_element_type | solution.py:197
  1.6 1.3 %fusion.200 = (s32[1]{0:T(128)}, s32[1]{0:T(128)}) fusion(s32[2]{0:T(128)} %param.43), kind=kLoop, calls=%fused_computation.305 | loop fusion | bytes 16 | tf_op jit(solution)/shard_map/slice | solution.py:196
  3.6 14.5 %conditional.8 = (bf16[400,128]{1,0:T(8,128)(2,1)}, bf16[400,128]{1,0:T(8,128)(2,1)}, bf16[400,128]{1,0:T(8,128)(2,1)}) conditional(s32[]{:T(128)} %bitcast.2, bf16[400,128]{1,0:T(8,128)(2,1)S(1)} %bitcast_convert_fusion, bf16[400,128]{1,0:T(8,128)(2,1)S(1)} %bitcast_convert_fusion, ...), branch_computations={%region_0.0_spmd, %region_1.0_spmd, %region_2.0_spmd, %region_3.0_... | conditional | bytes 1228944 | solution.py:57
  3.6 6.1 %collective-permute-start.18 = (bf16[400,128]{1,0:T(8,128)(2,1)S(1)}, bf16[400,128]{1,0:T(8,128)(2,1)}, u32[]{:S(2)}, u32[]{:S(2)}) collective-permute-start(bf16[400,128]{1,0:T(8,128)(2,1)S(1)} %param.6), channel_id=1, source_target_pairs={{0,28},{1,29},{2,30},{3,31},{4,24},{5,25},{6,26},{7,27},{8,20},{9,... | collective-permute-start | bytes 307208 | tf_op jit(solution)/shard_map/cond/branch_6_fun/ppermute | solution.py:18
  9.7 1.1 %collective-permute-start.19 = (bf16[400,128]{1,0:T(8,128)(2,1)S(1)}, bf16[400,128]{1,0:T(8,128)(2,1)}, u32[]{:S(2)}, u32[]{:S(2)}) collective-permute-start(bf16[400,128]{1,0:T(8,128)(2,1)S(1)} %param.6), channel_id=1, source_target_pairs={{0,30},{1,31},{2,28},{3,29},{4,26},{5,27},{6,24},{7,25},{8,22},{9,... | collective-permute-start | bytes 307208 | tf_op jit(solution)/shard_map/cond/branch_6_fun/ppermute | solution.py:18
  11.3 1.7 %collective-permute-done.18 = bf16[400,128]{1,0:T(8,128)(2,1)} collective-permute-done((bf16[400,128]{1,0:T(8,128)(2,1)S(1)}, bf16[400,128]{1,0:T(8,128)(2,1)}, u32[]{:S(2)}, u32[]{:S(2)}) %collective-permute-start.18) | collective-permute-done | bytes 102432 | tf_op jit(solution)/shard_map/cond/branch_6_fun/ppermute | solution.py:18
  13.0 5.1 %collective-permute-done.19 = bf16[400,128]{1,0:T(8,128)(2,1)} collective-permute-done((bf16[400,128]{1,0:T(8,128)(2,1)S(1)}, bf16[400,128]{1,0:T(8,128)(2,1)}, u32[]{:S(2)}, u32[]{:S(2)}) %collective-permute-start.19) | collective-permute-done | bytes 102432 | tf_op jit(solution)/shard_map/cond/branch_6_fun/ppermute | solution.py:18
  18.1 1.1 %fusion.95 = bf16[400,512]{1,0:T(8,128)(2,1)S(1)} fusion(bf16[400,128]{1,0:T(8,128)(2,1)S(1)} %bitcast_convert_fusion, bf16[400,128]{1,0:T(8,128)(2,1)} %get-tuple-element.180, bf16[400,128]{1,0:T(8,128)(2,1)} %get-tuple-element.179, bf16[400,128]{1,0:T(8,128)(2,1)} %get-tuple-element.178), kind=kLoop, calls=%fused_computation.155 | loop fusion | flops 1638400 | bytes 819200 | tf_op jit(solution)/shard_map/concatenate | solution.py:72
  19.3 0.7 broadcast_xor_fusion
  20.0 0.7 broadcast_xor_fusion.1
  20.7 0.7 fusion.198
  21.4 1.4 %fusion.199 = (s32[1,1,1]{0,2,1:T(1,128)}, s32[1,1,1]{0,2,1:T(1,128)}) fusion(s32[2,1,1]{0,2,1:T(1,128)} %param.42), kind=kLoop, calls=%fused_computation.304 | loop fusion | bytes 16 | tf_op jit(solution)/shard_map/slice | solution.py:207
  22.7 0.6 fusion.161
  23.9 1.6 %fusion.201 = (bf16[400,1024]{1,0:T(8,128)(2,1)S(1)}, f32[400,1024]{1,0:T(8,128)S(1)}) fusion(s32[1024]{0:T(1024)S(1)} %pad_add_fusion, bf16[400,128]{1,0:T(8,128)(2,1)S(1)} %bitcast_convert_fusion, bf16[400,128]{1,0:T(8,128)(2,1)S(1)} %get-tuple-element.244, bf16[400,128]{1,0:T(8,128)(2,1)} %get-tuple-element.178, bf16[400,128]{1,0:T(8,128)(2,1)S(1)} %get-tuple-element.245), kind=kOutput, calls=%fused_computation.306 | convolution fusion | flops 422002688 | bytes 2871296 | tf_op jit(solution)/shard_map/dot_general | solution.py:134
  25.7 1.6 %fusion.202 = (bf16[400,1024]{1,0:T(8,128)(2,1)S(1)}, f32[400,1024]{1,0:T(8,128)S(1)}) fusion(s32[1024]{0:T(1024)S(1)} %pad_add_fusion.1, bf16[400,128]{1,0:T(8,128)(2,1)S(1)} %get-tuple-element.243, bf16[400,128]{1,0:T(8,128)(2,1)} %get-tuple-element.180, bf16[400,128]{1,0:T(8,128)(2,1)S(1)} %get-tuple-element.242, bf16[400,128]{1,0:T(8,128)(2,1)} %get-tuple-element.179), kind=kOutput, calls=%fused_computation.307 | convolution fusion | flops 422002688 | bytes 2871296 | tf_op jit(solution)/shard_map/dot_general | solution.py:134
  27.5 0.7 negate_select_fusion.1
  32.0 0.6 fusion.204
  32.6 0.6 fusion.203
  34.7 0.6 fusion.160
  35.6 12.7 %conditional.12 = (bf16[400,128]{1,0:T(8,128)(2,1)}, f32[400,128]{1,0:T(8,128)S(1)}, bf16[400,128]{1,0:T(8,128)(2,1)}) conditional(s32[]{:T(128)} %bitcast.2, (bf16[400,128]{1,0:T(8,128)(2,1)S(1)}, bf16[400,128]{1,0:T(8,128)(2,1)S(1)}, bf16[400,128]{1,0:T(8,128)(2,1)S(1)}) %tuple.208, ...), branch_computations={%region_8.0_spmd, %region_9.0_spmd, %region_10.0_spmd, %region_11.... | conditional | flops 153600 | bytes 1638544
  35.6 3.1 %collective-permute-start.60 = (bf16[400,128]{1,0:T(8,128)(2,1)S(1)}, bf16[400,128]{1,0:T(8,128)(2,1)}, u32[]{:S(2)}, u32[]{:S(2)}) collective-permute-start(bf16[400,128]{1,0:T(8,128)(2,1)S(1)} %get-tuple-element.142), channel_id=1, source_target_pairs={{0,28},{1,29},{2,30},{3,31},{4,24},{5,25},{6,26},{7,27},{8,20},{9,... | collective-permute-start | bytes 307208 | tf_op jit(solution)/shard_map/cond/branch_6_fun/ppermute | solution.py:18
  38.7 2.6 %collective-permute-start.61 = (bf16[400,128]{1,0:T(8,128)(2,1)S(1)}, bf16[400,128]{1,0:T(8,128)(2,1)S(1)}, u32[]{:S(2)}, u32[]{:S(2)}) collective-permute-start(bf16[400,128]{1,0:T(8,128)(2,1)S(1)} %get-tuple-element.143), channel_id=1, source_target_pairs={{0,30},{1,31},{2,28},{3,29},{4,26},{5,27},{6,24},{7,25},{8,22},{9,... | collective-permute-start | bytes 307208 | tf_op jit(solution)/shard_map/cond/branch_6_fun/ppermute | solution.py:18
  41.9 1.9 %collective-permute-done.60 = bf16[400,128]{1,0:T(8,128)(2,1)} collective-permute-done((bf16[400,128]{1,0:T(8,128)(2,1)S(1)}, bf16[400,128]{1,0:T(8,128)(2,1)}, u32[]{:S(2)}, u32[]{:S(2)}) %collective-permute-start.60) | collective-permute-done | bytes 102432 | tf_op jit(solution)/shard_map/cond/branch_6_fun/ppermute | solution.py:18
  43.8 3.5 %collective-permute-done.61 = bf16[400,128]{1,0:T(8,128)(2,1)S(1)} collective-permute-done((bf16[400,128]{1,0:T(8,128)(2,1)S(1)}, bf16[400,128]{1,0:T(8,128)(2,1)S(1)}, u32[]{:S(2)}, u32[]{:S(2)}) %collective-permute-start.61) | collective-permute-done | bytes 102432 | tf_op jit(solution)/shard_map/cond/branch_6_fun/ppermute | solution.py:18
  47.3 0.9 convert_add_fusion.6
  48.2 1.0 %multiply_reduce_fusion.1 = (f32[128]{0:T(128)S(1)}, f32[400,128]{1,0:T(8,128)S(1)}) fusion(f32[400,128]{1,0:T(8,128)S(1)} %get-tuple-element.182, bf16[400,128]{1,0:T(8,128)(2,1)} %get-tuple-element.193, f32[400,512]{1,0:T(8,128)S(1)} %convert_element_type.296, f32[400,512]{1,0:T(8,128)S(1)} %get-tuple-element.269), kind=kLoop, calls=%fused_computation.234 | loop fusion | flops 307072 | bytes 922112 | tf_op jit(solution)/shard_map/reduce_sum | solution.py:210
  49.3 15.4 %conditional.10 = (bf16[400,128]{1,0:T(8,128)(2,1)}, bf16[400,128]{1,0:T(8,128)(2,1)}, bf16[400,128]{1,0:T(8,128)(2,1)}) conditional(s32[]{:T(128)} %bitcast.8, bf16[400,128]{1,0:T(8,128)(2,1)S(1)} %fusion.175, bf16[400,128]{1,0:T(8,128)(2,1)S(1)} %fusion.175, bf16[400,128]{1,0:T(8,128)(2,1)S(1)} %fusion.175, ...), branch_computations={%region_16.0_spmd, %region_17.0_spmd, %region_18.0_spmd, %region_1... | conditional | bytes 1228944 | solution.py:57
  49.4 4.8 %collective-permute-start.33 = (bf16[400,128]{1,0:T(8,128)(2,1)S(1)}, bf16[400,128]{1,0:T(8,128)(2,1)}, u32[]{:S(2)}, u32[]{:S(2)}) collective-permute-start(bf16[400,128]{1,0:T(8,128)(2,1)S(1)} %param.18), channel_id=1, source_target_pairs={{0,20},{1,21},{2,22},{3,23},{4,16},{5,17},{6,18},{7,19},{8,28},{9,... | collective-permute-start | bytes 307208 | tf_op jit(solution)/shard_map/cond/branch_4_fun/ppermute | solution.py:18
  54.2 1.0 %collective-permute-start.34 = (bf16[400,128]{1,0:T(8,128)(2,1)S(1)}, bf16[400,128]{1,0:T(8,128)(2,1)}, u32[]{:S(2)}, u32[]{:S(2)}) collective-permute-start(bf16[400,128]{1,0:T(8,128)(2,1)S(1)} %param.18), channel_id=1, source_target_pairs={{0,22},{1,23},{2,20},{3,21},{4,18},{5,19},{6,16},{7,17},{8,30},{9,... | collective-permute-start | bytes 307208 | tf_op jit(solution)/shard_map/cond/branch_4_fun/ppermute | solution.py:18
  55.2 0.6 collective-permute-start.35
  55.7 6.6 %collective-permute-done.33 = bf16[400,128]{1,0:T(8,128)(2,1)} collective-permute-done((bf16[400,128]{1,0:T(8,128)(2,1)S(1)}, bf16[400,128]{1,0:T(8,128)(2,1)}, u32[]{:S(2)}, u32[]{:S(2)}) %collective-permute-start.33) | collective-permute-done | bytes 102432 | tf_op jit(solution)/shard_map/cond/branch_4_fun/ppermute | solution.py:18
  62.4 2.3 %collective-permute-done.34 = bf16[400,128]{1,0:T(8,128)(2,1)} collective-permute-done((bf16[400,128]{1,0:T(8,128)(2,1)S(1)}, bf16[400,128]{1,0:T(8,128)(2,1)}, u32[]{:S(2)}, u32[]{:S(2)}) %collective-permute-start.34) | collective-permute-done | bytes 102432 | tf_op jit(solution)/shard_map/cond/branch_4_fun/ppermute | solution.py:18
  64.7 1.1 %fusion.90 = bf16[400,512]{1,0:T(8,128)(2,1)S(1)} fusion(bf16[400,128]{1,0:T(8,128)(2,1)S(1)} %fusion.175, bf16[400,128]{1,0:T(8,128)(2,1)} %get-tuple-element.185, bf16[400,128]{1,0:T(8,128)(2,1)} %get-tuple-element.184, bf16[400,128]{1,0:T(8,128)(2,1)} %get-tuple-element.183), kind=kLoop, calls=%fused_computation.151 | loop fusion | flops 1638400 | bytes 819200 | tf_op jit(solution)/shard_map/concatenate | solution.py:72
  66.2 1.4 %collective-permute-done.86 = bf16[400,512]{1,0:T(8,128)(2,1)S(1)} collective-permute-done((bf16[400,512]{1,0:T(8,128)(2,1)S(1)}, bf16[400,512]{1,0:T(8,128)(2,1)S(1)}, u32[]{:S(2)}, u32[]{:S(2)}) %collective-permute-start.86) | collective-permute-done | bytes 409632 | tf_op jit(solution)/shard_map/ppermute | solution.py:18
  67.6 1.5 %fusion.205 = (bf16[400,1024]{1,0:T(8,128)(2,1)S(1)}, f32[400,1024]{1,0:T(8,128)S(1)}) fusion(s32[1024]{0:T(1024)S(1)} %pad_add_fusion.2, bf16[400,128]{1,0:T(8,128)(2,1)S(1)} %fusion.175, bf16[400,128]{1,0:T(8,128)(2,1)S(1)} %get-tuple-element.236, bf16[400,128]{1,0:T(8,128)(2,1)} %get-tuple-element.183, bf16[400,128]{1,0:T(8,128)(2,1)S(1)} %get-tuple-element.237), kind=kOutput, calls=%fused_computation.310 | convolution fusion | flops 422002688 | bytes 2871296 | tf_op jit(solution)/shard_map/dot_general | solution.py:134
  69.4 1.6 %fusion.206 = (bf16[400,1024]{1,0:T(8,128)(2,1)S(1)}, f32[400,1024]{1,0:T(8,128)S(1)}) fusion(s32[1024]{0:T(1024)S(1)} %pad_add_fusion.3, bf16[400,128]{1,0:T(8,128)(2,1)S(1)} %get-tuple-element.235, bf16[400,128]{1,0:T(8,128)(2,1)} %get-tuple-element.185, bf16[400,128]{1,0:T(8,128)(2,1)S(1)} %get-tuple-element.234, bf16[400,128]{1,0:T(8,128)(2,1)} %get-tuple-element.184), kind=kOutput, calls=%fused_computation.311 | convolution fusion | flops 422002688 | bytes 2871296 | tf_op jit(solution)/shard_map/dot_general | solution.py:134
  71.2 0.6 negate_select_fusion
  75.7 0.6 fusion.208
  76.3 0.7 fusion.207
  77.3 1.6 %collective-permute-done.87 = bf16[400,512]{1,0:T(8,128)(2,1)S(1)} collective-permute-done((bf16[400,512]{1,0:T(8,128)(2,1)S(1)}, bf16[400,512]{1,0:T(8,128)(2,1)S(1)}, u32[]{:S(2)}, u32[]{:S(2)}) %collective-permute-start.87) | collective-permute-done | bytes 409632 | tf_op jit(solution)/shard_map/ppermute | solution.py:18
  79.1 12.8 %conditional.13 = (bf16[400,128]{1,0:T(8,128)(2,1)}, f32[400,128]{1,0:T(8,128)S(1)}, bf16[400,128]{1,0:T(8,128)(2,1)}) conditional(s32[]{:T(128)} %bitcast.8, (bf16[400,128]{1,0:T(8,128)(2,1)S(1)}, bf16[400,128]{1,0:T(8,128)(2,1)S(1)}, bf16[400,128]{1,0:T(8,128)(2,1)S(1)}) %tuple.209, ...), branch_computations={%region_24.0_spmd, %region_25.0_spmd, %region_26.0_spmd, %region_2... | conditional | flops 153600 | bytes 1638544
  79.2 3.8 %collective-permute-start.76 = (bf16[400,128]{1,0:T(8,128)(2,1)S(1)}, bf16[400,128]{1,0:T(8,128)(2,1)S(1)}, u32[]{:S(2)}, u32[]{:S(2)}) collective-permute-start(bf16[400,128]{1,0:T(8,128)(2,1)S(1)} %get-tuple-element.158), channel_id=1, source_target_pairs={{0,22},{1,23},{2,20},{3,21},{4,18},{5,19},{6,16},{7,17},{8,30},{9,... | collective-permute-start | bytes 307208 | tf_op jit(solution)/shard_map/cond/branch_4_fun/ppermute | solution.py:18
  83.0 1.5 %collective-permute-start.77 = (bf16[400,128]{1,0:T(8,128)(2,1)S(1)}, bf16[400,128]{1,0:T(8,128)(2,1)}, u32[]{:S(2)}, u32[]{:S(2)}) collective-permute-start(bf16[400,128]{1,0:T(8,128)(2,1)S(1)} %get-tuple-element.159), channel_id=1, source_target_pairs={{0,2},{1,3},{2,0},{3,1},{4,6},{5,7},{6,4},{7,5},{8,10},{9,11},{10,... | collective-permute-start | bytes 307208 | tf_op jit(solution)/shard_map/cond/branch_4_fun/ppermute | solution.py:18
  84.5 4.6 %collective-permute-done.75 = bf16[400,128]{1,0:T(8,128)(2,1)} collective-permute-done((bf16[400,128]{1,0:T(8,128)(2,1)S(1)}, bf16[400,128]{1,0:T(8,128)(2,1)}, u32[]{:S(2)}, u32[]{:S(2)}) %collective-permute-start.75) | collective-permute-done | bytes 102432 | tf_op jit(solution)/shard_map/cond/branch_4_fun/ppermute | solution.py:18
  89.1 1.9 %collective-permute-done.76 = bf16[400,128]{1,0:T(8,128)(2,1)S(1)} collective-permute-done((bf16[400,128]{1,0:T(8,128)(2,1)S(1)}, bf16[400,128]{1,0:T(8,128)(2,1)S(1)}, u32[]{:S(2)}, u32[]{:S(2)}) %collective-permute-start.76) | collective-permute-done | bytes 102432 | tf_op jit(solution)/shard_map/cond/branch_4_fun/ppermute | solution.py:18
  90.9 0.9 convert_add_fusion.11
  91.9 1.0 %multiply_reduce_fusion = (f32[128]{0:T(128)S(1)}, f32[400,128]{1,0:T(8,128)S(1)}) fusion(f32[400,128]{1,0:T(8,128)S(1)} %get-tuple-element.187, bf16[400,128]{1,0:T(8,128)(2,1)} %get-tuple-element.197, f32[400,512]{1,0:T(8,128)S(1)} %convert_element_type.313, f32[400,512]{1,0:T(8,128)S(1)} %get-tuple-element.277), kind=kLoop, calls=%fused_computation.233 | loop fusion | flops 307072 | bytes 922112 | tf_op jit(solution)/shard_map/reduce_sum | solution.py:210
  93.4 0.7 subtract_bitcast_fusion
  (83 shorter events, 12.4 us)
Async XLA Ops:
  0.6 22.8 %copy-start = (bf16[256,400]{0,1:T(8,128)(2,1)S(1)}, bf16[256,400]{0,1:T(8,128)(2,1)}, u32[]{:S(2)}) copy-start(bf16[256,400]{0,1:T(8,128)(2,1)} %param.38) | copy-start | bytes 614404
  3.6 9.4 %collective-permute-start.18 = (bf16[400,128]{1,0:T(8,128)(2,1)S(1)}, bf16[400,128]{1,0:T(8,128)(2,1)}, u32[]{:S(2)}, u32[]{:S(2)}) collective-permute-start(bf16[400,128]{1,0:T(8,128)(2,1)S(1)} %param.6), channel_id=1, source_target_pairs={{0,28},{1,29},{2,30},{3,31},{4,24},{5,25},{6,26},{7,27},{8,20},{9,... | collective-permute-start | bytes 307208 | tf_op jit(solution)/shard_map/cond/branch_6_fun/ppermute | solution.py:18
  9.7 8.4 %collective-permute-start.19 = (bf16[400,128]{1,0:T(8,128)(2,1)S(1)}, bf16[400,128]{1,0:T(8,128)(2,1)}, u32[]{:S(2)}, u32[]{:S(2)}) collective-permute-start(bf16[400,128]{1,0:T(8,128)(2,1)S(1)} %param.6), channel_id=1, source_target_pairs={{0,30},{1,31},{2,28},{3,29},{4,26},{5,27},{6,24},{7,25},{8,22},{9,... | collective-permute-start | bytes 307208 | tf_op jit(solution)/shard_map/cond/branch_6_fun/ppermute | solution.py:18
  10.8 7.3 %collective-permute-start.20 = (bf16[400,128]{1,0:T(8,128)(2,1)S(1)}, bf16[400,128]{1,0:T(8,128)(2,1)}, u32[]{:S(2)}, u32[]{:S(2)}) collective-permute-start(bf16[400,128]{1,0:T(8,128)(2,1)S(1)} %param.6), channel_id=1, source_target_pairs={{0,2},{1,3},{2,0},{3,1},{4,6},{5,7},{6,4},{7,5},{8,10},{9,11},{10,... | collective-permute-start | bytes 307208 | tf_op jit(solution)/shard_map/cond/branch_6_fun/ppermute | solution.py:18
  19.2 4.6 %collective-permute-start.84 = (bf16[400,512]{1,0:T(8,128)(2,1)S(1)}, bf16[400,512]{1,0:T(8,128)(2,1)S(1)}, u32[]{:S(2)}, u32[]{:S(2)}) collective-permute-start(bf16[400,512]{1,0:T(8,128)(2,1)S(1)} %fusion.95), channel_id=1, source_target_pairs={{0,1},{1,0},{2,3},{3,2},{4,5},{5,4},{6,7},{7,6},{8,9},{9,8},{10,11... | collective-permute-start | bytes 1228808 | tf_op jit(solution)/shard_map/ppermute | solution.py:18
  33.4 1.9 %collective-permute-start.85 = (bf16[400,512]{1,0:T(8,128)(2,1)S(1)}, bf16[400,512]{1,0:T(8,128)(2,1)S(1)}, u32[]{:S(2)}, u32[]{:S(2)}) collective-permute-start(bf16[400,512]{1,0:T(8,128)(2,1)S(1)} %pad_maximum_fusion.8), channel_id=1, source_target_pairs={{0,1},{1,0},{2,3},{3,2},{4,5},{5,4},{6,7},{7,6},{8,9},{9,8},{10,11... | collective-permute-start | bytes 1228808 | tf_op jit(solution)/shard_map/ppermute | solution.py:18
  35.6 13.7 %copy-start.2 = (f32[128]{0:T(128)S(1)}, f32[128]{0:T(128)}, u32[]{:S(2)}) copy-start(f32[128]{0:T(128)} %param.37) | copy-start | bytes 1540
  35.6 13.7 %copy-start.1 = (f32[128,400]{0,1:T(8,128)S(1)}, f32[128,400]{0,1:T(8,128)}, u32[]{:S(2)}) copy-start(f32[128,400]{0,1:T(8,128)} %param.36) | copy-start | bytes 614404
  35.6 8.1 %collective-permute-start.60 = (bf16[400,128]{1,0:T(8,128)(2,1)S(1)}, bf16[400,128]{1,0:T(8,128)(2,1)}, u32[]{:S(2)}, u32[]{:S(2)}) collective-permute-start(bf16[400,128]{1,0:T(8,128)(2,1)S(1)} %get-tuple-element.142), channel_id=1, source_target_pairs={{0,28},{1,29},{2,30},{3,31},{4,24},{5,25},{6,26},{7,27},{8,20},{9,... | collective-permute-start | bytes 307208 | tf_op jit(solution)/shard_map/cond/branch_6_fun/ppermute | solution.py:18
  38.7 8.6 %collective-permute-start.61 = (bf16[400,128]{1,0:T(8,128)(2,1)S(1)}, bf16[400,128]{1,0:T(8,128)(2,1)S(1)}, u32[]{:S(2)}, u32[]{:S(2)}) collective-permute-start(bf16[400,128]{1,0:T(8,128)(2,1)S(1)} %get-tuple-element.143), channel_id=1, source_target_pairs={{0,30},{1,31},{2,28},{3,29},{4,26},{5,27},{6,24},{7,25},{8,22},{9,... | collective-permute-start | bytes 307208 | tf_op jit(solution)/shard_map/cond/branch_6_fun/ppermute | solution.py:18
  41.3 6.9 %collective-permute-start.62 = (bf16[400,128]{1,0:T(8,128)(2,1)S(1)}, bf16[400,128]{1,0:T(8,128)(2,1)}, u32[]{:S(2)}, u32[]{:S(2)}) collective-permute-start(bf16[400,128]{1,0:T(8,128)(2,1)S(1)} %get-tuple-element.144), channel_id=1, source_target_pairs={{0,2},{1,3},{2,0},{3,1},{4,6},{5,7},{6,4},{7,5},{8,10},{9,11},{10,... | collective-permute-start | bytes 307208 | tf_op jit(solution)/shard_map/cond/branch_6_fun/ppermute | solution.py:18
  49.4 13.0 %collective-permute-start.33 = (bf16[400,128]{1,0:T(8,128)(2,1)S(1)}, bf16[400,128]{1,0:T(8,128)(2,1)}, u32[]{:S(2)}, u32[]{:S(2)}) collective-permute-start(bf16[400,128]{1,0:T(8,128)(2,1)S(1)} %param.18), channel_id=1, source_target_pairs={{0,20},{1,21},{2,22},{3,23},{4,16},{5,17},{6,18},{7,19},{8,28},{9,... | collective-permute-start | bytes 307208 | tf_op jit(solution)/shard_map/cond/branch_4_fun/ppermute | solution.py:18
  54.2 10.5 %collective-permute-start.34 = (bf16[400,128]{1,0:T(8,128)(2,1)S(1)}, bf16[400,128]{1,0:T(8,128)(2,1)}, u32[]{:S(2)}, u32[]{:S(2)}) collective-permute-start(bf16[400,128]{1,0:T(8,128)(2,1)S(1)} %param.18), channel_id=1, source_target_pairs={{0,22},{1,23},{2,20},{3,21},{4,18},{5,19},{6,16},{7,17},{8,30},{9,... | collective-permute-start | bytes 307208 | tf_op jit(solution)/shard_map/cond/branch_4_fun/ppermute | solution.py:18
  55.2 9.5 %collective-permute-start.35 = (bf16[400,128]{1,0:T(8,128)(2,1)S(1)}, bf16[400,128]{1,0:T(8,128)(2,1)}, u32[]{:S(2)}, u32[]{:S(2)}) collective-permute-start(bf16[400,128]{1,0:T(8,128)(2,1)S(1)} %param.18), channel_id=1, source_target_pairs={{0,2},{1,3},{2,0},{3,1},{4,6},{5,7},{6,4},{7,5},{8,10},{9,11},{10,... | collective-permute-start | bytes 307208 | tf_op jit(solution)/shard_map/cond/branch_4_fun/ppermute | solution.py:18
  65.7 1.8 %collective-permute-start.86 = (bf16[400,512]{1,0:T(8,128)(2,1)S(1)}, bf16[400,512]{1,0:T(8,128)(2,1)S(1)}, u32[]{:S(2)}, u32[]{:S(2)}) collective-permute-start(bf16[400,512]{1,0:T(8,128)(2,1)S(1)} %fusion.90), channel_id=1, source_target_pairs={{0,1},{1,0},{2,3},{3,2},{4,5},{5,4},{6,7},{7,6},{8,9},{9,8},{10,11... | collective-permute-start | bytes 1228808 | tf_op jit(solution)/shard_map/ppermute | solution.py:18
  77.1 1.8 %collective-permute-start.87 = (bf16[400,512]{1,0:T(8,128)(2,1)S(1)}, bf16[400,512]{1,0:T(8,128)(2,1)S(1)}, u32[]{:S(2)}, u32[]{:S(2)}) collective-permute-start(bf16[400,512]{1,0:T(8,128)(2,1)S(1)} %pad_maximum_fusion.9), channel_id=1, source_target_pairs={{0,1},{1,0},{2,3},{3,2},{4,5},{5,4},{6,7},{7,6},{8,9},{9,8},{10,11... | collective-permute-start | bytes 1228808 | tf_op jit(solution)/shard_map/ppermute | solution.py:18
  79.1 9.9 %collective-permute-start.75 = (bf16[400,128]{1,0:T(8,128)(2,1)S(1)}, bf16[400,128]{1,0:T(8,128)(2,1)}, u32[]{:S(2)}, u32[]{:S(2)}) collective-permute-start(bf16[400,128]{1,0:T(8,128)(2,1)S(1)} %get-tuple-element.157), channel_id=1, source_target_pairs={{0,20},{1,21},{2,22},{3,23},{4,16},{5,17},{6,18},{7,19},{8,28},{9,... | collective-permute-start | bytes 307208 | tf_op jit(solution)/shard_map/cond/branch_4_fun/ppermute | solution.py:18
  79.2 11.7 %collective-permute-start.76 = (bf16[400,128]{1,0:T(8,128)(2,1)S(1)}, bf16[400,128]{1,0:T(8,128)(2,1)S(1)}, u32[]{:S(2)}, u32[]{:S(2)}) collective-permute-start(bf16[400,128]{1,0:T(8,128)(2,1)S(1)} %get-tuple-element.158), channel_id=1, source_target_pairs={{0,22},{1,23},{2,20},{3,21},{4,18},{5,19},{6,16},{7,17},{8,30},{9,... | collective-permute-start | bytes 307208 | tf_op jit(solution)/shard_map/cond/branch_4_fun/ppermute | solution.py:18
  83.0 8.9 %collective-permute-start.77 = (bf16[400,128]{1,0:T(8,128)(2,1)S(1)}, bf16[400,128]{1,0:T(8,128)(2,1)}, u32[]{:S(2)}, u32[]{:S(2)}) collective-permute-start(bf16[400,128]{1,0:T(8,128)(2,1)S(1)} %get-tuple-element.159), channel_id=1, source_target_pairs={{0,2},{1,3},{2,0},{3,1},{4,6},{5,7},{6,4},{7,5},{8,10},{9,11},{10,... | collective-permute-start | bytes 307208 | tf_op jit(solution)/shard_map/cond/branch_4_fun/ppermute | solution.py:18
